TPU v7x, 256 devices: a whole 4x4x8 slice. The times are simulated.
256 devices in a mesh: ta: 8 (over x, core), tb: 32 (over z, y).
Axes of the slice: x: 4, y: 4, z: 8, core: 2. Of those that a mesh axis runs over, the one named last changes fastest.
Arguments:
- theta_cube: bfloat16 [256, 90, 32768], P(('ta', 'tb')), may hold values from -20 to 20, as said below
- station_permutation_map: int32 [1024], replicated, may hold values from 0 to 1023, each once
- station_bathymetry_group: int32 [32768], replicated, may hold values from 0 to 15
- baroclinic_basis: bfloat16 [16, 90, 90], replicated, may hold values from -0.625 to 0.625
Outputs:
- anomaly_coef: bfloat16 [90, 256, 32768], P(None, None, ('ta', 'tb'))
Inputs may be any that keep to these rules, and one draw needn't show every extreme that they name: `theta_cube`: temperature is a level-and-column profile plus time variation.
All inputs are finite; a program needn't handle non-finite values.
Results may differ from a plain program's by a relative error of at most 0.001.
Values may be sent and summed in bfloat16 or wider, within the bound.
A program may use at most 128 MiB of HBM per device.

v0:
```python
import jax
import jax.numpy as jnp
from jax import lax
from jax.sharding import PartitionSpec as P

TILE = 32


def cut_along(shard, dim, devices):
    before, after = (shard.shape[:dim], shard.shape[dim + 1 :])
    return jnp.moveaxis(shard.reshape(*before, devices, -1, *after), dim, 0)


def joined_along(pieces, dim):
    pieces = jnp.moveaxis(pieces, 0, dim)
    lengths = pieces.shape
    return pieces.reshape(*lengths[:dim], lengths[dim] * lengths[dim + 1], *lengths[dim + 2 :])


def one_exchange(shard, axis, axes, splits, concats):
    sizes = [lax.axis_size(a) for a in axes]
    pieces = cut_along(shard, splits[0], sizes[0])
    pieces = jnp.moveaxis(cut_along(pieces, splits[1] + 1, sizes[1]), 0, 1)
    inside = pieces.shape[2:]
    pieces = pieces.reshape(-1, *inside)
    pieces = lax.all_to_all(pieces, axis, split_axis=0, concat_axis=0, tiled=True)
    pieces = joined_along(pieces.reshape(*sizes, *inside), concats[0] + 1)
    return joined_along(pieces, concats[1])


def on_device(theta_cube, station_permutation_map, station_bathymetry_group, baroclinic_basis):
    instant_portion, vertical_grid_count, ocean_stations = theta_cube.shape
    classes, _, mode_count = baroclinic_basis.shape
    size_ta = lax.axis_size("ta")
    size_tb = lax.axis_size("tb")
    devices = size_ta * size_tb
    col_dev = ocean_stations // devices
    group_count = ocean_stations // TILE
    owner = lax.axis_index("ta") * size_tb + lax.axis_index("tb")
    grouped = theta_cube.reshape(instant_portion, vertical_grid_count, group_count, TILE)
    regrouped_stations = jnp.take(grouped, station_permutation_map, axis=2).reshape(
        instant_portion, vertical_grid_count, devices, col_dev
    )
    my_groups = lax.dynamic_slice_in_dim(
        station_permutation_map, owner * (col_dev // TILE), col_dev // TILE
    )
    my_columns = (my_groups[:, None] * TILE + jnp.arange(TILE, dtype=jnp.int32)[None, :]).reshape(
        col_dev
    )
    local_category = jnp.take(station_bathymetry_group, my_columns, axis=0)
    one_hot = (local_category[:, None] == jnp.arange(classes, dtype=jnp.int32)[None, :]).astype(
        jnp.bfloat16
    )
    per_column = jnp.dot(
        one_hot,
        baroclinic_basis.reshape(classes, vertical_grid_count * mode_count),
        preferred_element_type=jnp.float32,
    )
    per_column = per_column.astype(jnp.bfloat16).reshape(col_dev, vertical_grid_count, mode_count)
    shaped = regrouped_stations.reshape(
        1, 1, instant_portion, vertical_grid_count, size_ta, size_tb, col_dev
    )
    moved = one_exchange(shaped, ("ta", "tb"), ("ta", "tb"), (4, 5), (0, 1))
    gathered = moved.reshape(devices * instant_portion, vertical_grid_count, col_dev)
    modal_amplitude = jnp.einsum(
        "btq,qtf->fbq", gathered, per_column, preferred_element_type=jnp.float32
    )
    mean_coef = jnp.mean(modal_amplitude, axis=1, keepdims=True)
    return (modal_amplitude - mean_coef).astype(jnp.bfloat16)


def solution(mesh):
    return jax.shard_map(
        on_device,
        mesh=mesh,
        in_specs=(P(("ta", "tb"), None, None), P(), P(), P()),
        out_specs=P(None, None, ("ta", "tb")),
        check_vma=False,
    )
```

profile of v0, /device:TPU:1, one launch (start us, length us, event | category | flops | bytes accessed | tf_op | source)
XLA Modules:
  0.0 231.5 jit_solution(5792061602108719480)
XLA Ops:
  0.0 0.7 compare_and_fusion
  0.7 0.7 fusion.2
  1.4 0.2 broadcast_in_dim.30
  1.6 0.3 broadcast_in_dim.31
  1.9 0.2 broadcast_in_dim.32
  2.1 10.2 %copy.15 = bf16[1,90,32768]{1,2,0:T(8,128)(2,1)} copy(bf16[1,90,32768]{2,1,0:T(8,128)(2,1)} %param.4) | data formatting | bytes 11796480 | tf_op args[0]
  12.3 13.2 %gather_fusion.1 = bf16[1024,90,32]{1,2,0:T(8,128)(2,1)} fusion(bf16[90,1024,32]{0,2,1:T(8,128)(2,1)} %bitcast.29, s32[1024]{0:T(1024)S(1)} %fusion.2), kind=kCustom, calls=%fused_computation.1 | custom fusion | bytes 11800576 | tf_op jit(solution)/shard_map/jit(_take)/gather | solution.py:41
  25.5 7.7 %broadcast_select_fusion = bf16[1,1,1,90,8,1,32,128]{3,7,6,4,5,2,1,0:T(8,128)(2,1)} fusion(bf16[1,1,1,90,8,1,32,128]{3,7,6,4,5,2,1,0:T(8,128)(2,1)} %bitcast.30, pred[8,32,128]{2,1,0:T(8,128)(4,1)S(1)} %broadcast_in_dim.32), kind=kLoop, calls=%fused_computation.6 | loop fusion | flops 2949120 | bytes 11829248 | tf_op jit(solution)/shard_map/jit(_take)/select_n | solution.py:41
  33.2 10.3 %copy.17 = bf16[256,1,1,1,90,1,1,128]{7,4,6,5,3,2,1,0:T(8,128)(2,1)} copy(bf16[256,1,1,1,90,1,1,128]{4,7,0,6,5,3,2,1:T(8,128)(2,1)} %bitcast.31) | data formatting | bytes 11796480 | tf_op jit(solution)/shard_map/reshape | solution.py:25
  43.6 16.5 %all-to-all-start = ((bf16[256,1,1,1,90,1,1,128]{7,4,6,5,3,2,1,0:T(8,128)(2,1)}), bf16[256,1,1,1,90,1,1,128]{7,4,6,5,3,2,1,0:T(8,128)(2,1)}, u32[]{:S(2)}, u32[]{:S(2)}) async-start(bf16[256,1,1,1,90,1,1,128]{7,4,6,5,3,2,1,0:T(8,128)(2,1)} %copy.17), calls=%async_computation | async-start | bytes 12582912 | tf_op jit(solution)/shard_map/all_to_all | solution.py:26
  60.1 0.8 dynamic-slice_multiply_fusion
  60.9 0.1 add.78
  61.0 0.1 add.75
  61.1 0.1 copy.14
  61.2 0.5 reshape.104
  61.7 1.1 gather_fusion
  62.9 1.3 convolution_convert_fusion
  64.2 1.9 reshape.105
  66.1 4.0 %copy.19 = bf16[128,90,90]{1,2,0:T(8,128)(2,1)S(1)} copy(bf16[128,90,90]{0,2,1:T(8,128)(2,1)} %reshape.105) | data formatting | bytes 4147200 | tf_op jit(solution)/shard_map/reshape | solution.py:59
  70.1 132.9 %all-to-all-done = bf16[256,1,1,1,90,1,1,128]{7,4,6,5,3,2,1,0:T(8,128)(2,1)} async-done(((bf16[256,1,1,1,90,1,1,128]{7,4,6,5,3,2,1,0:T(8,128)(2,1)}), bf16[256,1,1,1,90,1,1,128]{7,4,6,5,3,2,1,0:T(8,128)(2,1)}, u32[]{:S(2)}, u32[]{:S(2)}) %all-to-all-start) | async-done | bytes 5898272 | tf_op jit(solution)/shard_map/all_to_all | solution.py:26
  203.0 9.7 %copy.20 = bf16[256,90,128]{0,1,2:T(8,128)(2,1)} copy(bf16[256,90,128]{2,1,0:T(8,128)(2,1)} %bitcast.13) | data formatting | bytes 11796480 | tf_op jit(solution)/shard_map/reshape;reshape | solution.py:64
  212.8 5.6 %bitcast_reduce_fusion = (f32[90,128]{0,1:T(8,128)S(1)}, f32[128,90,256]{2,1,0:T(8,128)S(1)}) fusion(bf16[128,90,90]{1,2,0:T(8,128)(2,1)S(1)} %copy.19, bf16[256,90,128]{0,1,2:T(8,128)(2,1)} %copy.20), kind=kOutput, calls=%fused_computation.3 | convolution fusion | flops 533779200 | bytes 19814400 | tf_op jit(solution)/shard_map/btq,qtf->fbq/dot_general | solution.py:65
  218.4 4.0 %fusion = bf16[90,256,128]{1,0,2:T(8,128)(2,1)} fusion(f32[128,90,256]{2,1,0:T(8,128)S(1)} %get-tuple-element.6, f32[90,128]{0,1:T(8,128)S(1)} %broadcast_multiply_fusion), kind=kLoop, calls=%fused_computation.4 | loop fusion | flops 5898240 | bytes 17740800 | tf_op jit(solution)/shard_map/convert_element_type | solution.py:69
  222.4 9.1 %copy.21 = bf16[90,256,128]{2,1,0:T(8,128)(2,1)} copy(bf16[90,256,128]{1,0,2:T(8,128)(2,1)} %fusion) | data formatting | bytes 11796480 | tf_op jit(solution)/shard_map/convert_element_type | solution.py:69
  (9 shorter events, 0.1 us)
Async XLA Ops:
  0.0 61.7 %copy-start = (s32[32768]{0:T(1024)S(1)}, s32[32768]{0:T(1024)}, u32[]{:S(2)}) copy-start(s32[32768]{0:T(1024)} %param.6) | copy-start | bytes 393220
  43.6 17.5 %copy-start.1 = (bf16[16,90,90]{2,0,1:T(8,128)(2,1)S(1)}, bf16[16,90,90]{2,0,1:T(8,128)(2,1)}, u32[]{:S(2)}) copy-start(bf16[16,90,90]{2,0,1:T(8,128)(2,1)} %param.7) | copy-start | bytes 777604
  43.6 159.5 %all-to-all-start = ((bf16[256,1,1,1,90,1,1,128]{7,4,6,5,3,2,1,0:T(8,128)(2,1)}), bf16[256,1,1,1,90,1,1,128]{7,4,6,5,3,2,1,0:T(8,128)(2,1)}, u32[]{:S(2)}, u32[]{:S(2)}) async-start(bf16[256,1,1,1,90,1,1,128]{7,4,6,5,3,2,1,0:T(8,128)(2,1)} %copy.17), calls=%async_computation | async-start | bytes 12582912 | tf_op jit(solution)/shard_map/all_to_all | solution.py:26
where the time goes:
time: 233 us; the launch traced here: 232 us
  waiting for transfers between devices  133 us (57%)
  local copies, waits for them, and re-layouts  61.1 us (26%)
  starting transfers between devices  16.5 us (7%)
  other arithmetic  14 us (6%)
  matrix products  6.91 us (3%)
    all_to_all x1, waiting for transfers between devices, one_exchange(): lax.all_to_all(pieces, axis, split_axis=0, concat_axis=0, tiled=True)  133 us
    all_to_all x1, starting transfers between devices, one_exchange(): lax.all_to_all(pieces, axis, split_axis=0, concat_axis=0, tiled=True)  16.5 us
    gather x1, local copies, waits for them, and re-layouts, on_device(): jnp.take(grouped, station_permutation_map, axis=2)  13.2 us
    reshape x1, local copies, waits for them, and re-layouts, one_exchange(): pieces = pieces.reshape(-1, *inside)  10.3 us
    unnamed x6, local copies, waits for them, and re-layouts  10.3 us
    another operation x1, local copies, waits for them, and re-layouts, on_device(): moved.reshape(devices * instant_portion, vertical_grid_count, col_dev)  9.75 us
    convert_element_type x1, local copies, waits for them, and re-layouts, on_device(): return (modal_amplitude - mean_coef).astype(jnp.bfloat16)  9.14 us
    select_n x1, other arithmetic, on_device(): jnp.take(grouped, station_permutation_map, axis=2)  7.69 us
  transfers between devices with their start and end apart: 1, of which 1 were waited for; matrix products, arithmetic and copies ran while one was open for 4% of the time, Pallas kernels for 0%

commit v1 on v0

v1 whole, which is shorter than its diff:
```python
import jax
import jax.numpy as jnp
from jax import lax
from jax.experimental import pallas as pl
from jax.experimental.pallas import tpu as pltpu
from jax.sharding import PartitionSpec as P

TILE = 32
LANES = 128
MESH = pl.DeviceIdType.MESH


def place():
    ta, tb = lax.axis_index("ta"), lax.axis_index("tb")
    return ta // 2, ta % 2, tb % 4, tb // 4


def peer(step, sign):
    x, core, y, z = place()
    turn = (step // 2) % 8
    dz = jnp.where(turn % 2 == 1, 8 - (turn + 1) // 2, turn // 2 + 1)
    dz = jnp.where(turn == 7, 0, dz)
    dy, dx = (step // 16) % 4, (step // 64) % 4
    ta = ((x + sign * dx + 4) % 4) * 2 + (core + step) % 2
    tb = ((z + sign * dz + 8) % 8) * 4 + (y + sign * dy + 4) % 4
    return ta, tb


SELF = 14


def regroup_kernel(perm, mine, group, theta, out, kind):
    levels = theta.shape[0]
    first = pl.program_id(0) * out.shape[0]
    quarter = lax.broadcasted_iota(jnp.int32, (levels, LANES), 1) // TILE

    def gathered(t, which, read):
        block = None
        for k in range(4):
            g = perm[4 * t + k]
            part = read(g // 4)
            part = pltpu.roll(part, ((k - g % 4 + 4) % 4) * TILE, 1)
            block = part if block is None else jnp.where(which == k, part, block)
        return block

    def tile_of(tile):
        return theta[:, pl.ds(pl.multiple_of(tile * LANES, LANES), LANES)]

    for i in range(out.shape[0]):
        out[i, pl.ds(0, levels), :] = gathered(first + i, quarter, tile_of)

    @pl.when(pl.program_id(0) == 0)
    def _():
        kind[...] = gathered(mine[0], quarter[:1], lambda tile: group[pl.ds(tile, 1), :])


def exchange_kernel(
    kind, basis, outbox, coef, total, inbox, modes, load_sem, send_sem, recv_sem, stage_sem
):
    levels = basis.shape[1]
    classes = basis.shape[0]
    devices = outbox.shape[0]
    ta, tb = lax.axis_index("ta"), lax.axis_index("tb")
    me = ta * 32 + tb
    here = inbox.at[me, pl.ds(0, levels)]
    load = pltpu.make_async_copy(outbox.at[me, pl.ds(0, levels)], here, load_sem)
    load.start()

    barrier = pltpu.get_barrier_semaphore()
    for d in range(1, 8):
        pl.semaphore_signal(barrier, inc=1, device_id=((ta + d) % 8, tb), device_id_type=MESH)

    def greet(d, carry):
        pl.semaphore_signal(barrier, inc=1, device_id=(ta, (tb + d) % 32), device_id_type=MESH)
        return carry

    lax.fori_loop(1, 32, greet, 0)

    def send(step):
        a, b = peer(step, 1)
        t = a * 32 + b

        @pl.when(step != SELF)
        def _():
            pltpu.make_async_remote_copy(
                src_ref=outbox.at[t, pl.ds(0, levels)],
                dst_ref=inbox.at[me, pl.ds(0, levels)],
                send_sem=send_sem,
                recv_sem=recv_sem.at[me],
                device_id=(a, b),
                device_id_type=MESH,
            ).start()

    pl.semaphore_wait(barrier, 38)
    for d in range(1, 8):
        pl.semaphore_signal(stage_sem, inc=1, device_id=((ta + d) % 8, tb), device_id_type=MESH)
    pl.semaphore_wait(stage_sem, 7)

    def send_all(step, carry):
        send(step)
        return carry

    lax.fori_loop(0, devices, send_all, 0)

    for c in range(classes):
        modes[c] = basis[c].astype(jnp.float32).T.astype(jnp.bfloat16)
    total[...] = jnp.zeros_like(total)

    def project(s):
        found = inbox[s, pl.ds(0, levels), :]
        out = jnp.zeros((levels, LANES), jnp.float32)
        for c in range(classes):
            part = jnp.dot(modes[c], found, preferred_element_type=jnp.float32)
            out = jnp.where(kind[...] == c, part, out)
        coef[:, s, :] = out
        total[...] += out

    load.wait()
    project(me)

    def receive(step, carry):
        a, b = peer(step, -1)
        s = a * 32 + b

        @pl.when(step != SELF)
        def _():
            here = inbox.at[s, pl.ds(0, levels)]
            pltpu.make_async_copy(here, here, recv_sem.at[s]).wait()
            project(s)

        return carry

    lax.fori_loop(0, devices, receive, 0)
    sent = outbox.at[pl.ds(0, devices - 1), pl.ds(0, levels)]
    pltpu.make_async_copy(sent, sent, send_sem).wait()


def centre_kernel(coef, total, out):
    snaps = out.shape[1]
    for m in range(out.shape[0]):
        mean = total[pl.program_id(0) * out.shape[0] + m][None, :] * (1.0 / snaps)
        out[m] = (coef[m, pl.ds(0, snaps), :] - mean).astype(out.dtype)


def on_device(theta_cube, station_permutation_map, station_bathymetry_group, baroclinic_basis):
    _, levels, columns = theta_cube.shape
    classes, _, mode_count = baroclinic_basis.shape
    devices = columns // LANES
    snaps = devices
    vmem = pl.BlockSpec(memory_space=pltpu.VMEM)
    me = (lax.axis_index("ta") * 32 + lax.axis_index("tb")).astype(jnp.int32).reshape(1)
    smem = pl.BlockSpec(memory_space=pltpu.SMEM)
    step = 16
    blocks, kind = pl.pallas_call(
        regroup_kernel,
        grid=(devices // step,),
        out_shape=(
            jax.ShapeDtypeStruct((devices, 96, LANES), jnp.bfloat16),
            jax.ShapeDtypeStruct((1, LANES), jnp.int32),
        ),
        in_specs=[smem, smem, vmem, vmem],
        out_specs=(pl.BlockSpec((step, 96, LANES), lambda i: (i, 0, 0)), vmem),
        name="regroup",
    )(
        station_permutation_map,
        me,
        station_bathymetry_group.reshape(columns // LANES, LANES),
        theta_cube.reshape(levels, columns),
    )
    coef, total = pl.pallas_call(
        exchange_kernel,
        out_shape=(
            jax.ShapeDtypeStruct((mode_count, snaps + 8, LANES), jnp.float32),
            jax.ShapeDtypeStruct((mode_count, LANES), jnp.float32),
        ),
        in_specs=[vmem, vmem, pl.BlockSpec(memory_space=pl.ANY)],
        out_specs=(vmem, vmem),
        scratch_shapes=[
            pltpu.VMEM((devices, 96, LANES), jnp.bfloat16),
            pltpu.VMEM((classes, mode_count, levels), jnp.bfloat16),
            pltpu.SemaphoreType.DMA,
            pltpu.SemaphoreType.DMA,
            pltpu.SemaphoreType.DMA((devices,)),
            pltpu.SemaphoreType.REGULAR,
        ],
        compiler_params=pltpu.CompilerParams(
            collective_id=0, has_side_effects=True, vmem_limit_bytes=40 * 2**20
        ),
        name="exchange",
    )(kind, baroclinic_basis, blocks)
    rows = 9
    return pl.pallas_call(
        centre_kernel,
        grid=(mode_count // rows,),
        out_shape=jax.ShapeDtypeStruct((mode_count, snaps, LANES), jnp.bfloat16),
        in_specs=[pl.BlockSpec((rows, snaps + 8, LANES), lambda i: (i, 0, 0)), vmem],
        out_specs=pl.BlockSpec((rows, snaps, LANES), lambda i: (i, 0, 0)),
        name="centre",
    )(coef, total)


def solution(mesh):
    return jax.shard_map(
        on_device,
        mesh=mesh,
        in_specs=(P(("ta", "tb"), None, None), P(), P(), P()),
        out_specs=P(None, None, ("ta", "tb")),
        check_vma=False,
    )
```

time: 233 us -> 185 us (0.79)
  Pallas kernels: 0 us -> 176 us
  waiting for transfers between devices: 133 us -> 0 us
  local copies, waits for them, and re-layouts: 61.1 us -> 5.14 us
  starting transfers between devices: 16.5 us -> 0 us
  other arithmetic: 14 us -> 0 us
  matrix products: 6.91 us -> 0 us
    pallas_call x0 -> x3, Pallas kernels: none -> 176 us  [the longest x1 151 us: on_device(): pl.pallas_call(exchange_kernel, out_shape=(jax.ShapeDtypeStruct((mode_cou...]
    all_to_all x1 -> x0, waiting for transfers between devices: 133 us -> none  [one_exchange(): lax.all_to_all(pieces, axis, split_axis=0, concat_axis=0, tiled=True)]
    reshape x4 -> x0, local copies, waits for them, and re-layouts: 16.7 us -> none  [the longest x1 10.3 us: one_exchange(): pieces = pieces.reshape(-1, *inside)]
    all_to_all x1 -> x0, starting transfers between devices: 16.5 us -> none  [one_exchange(): lax.all_to_all(pieces, axis, split_axis=0, concat_axis=0, tiled=True)]
    gather x2 -> x0, local copies, waits for them, and re-layouts: 14.4 us -> none  [the longest x1 13.2 us: on_device(): jnp.take(grouped, station_permutation_map, axis=2)]
    another operation x1 -> x0, local copies, waits for them, and re-layouts: 9.75 us -> none  [on_device(): moved.reshape(devices * instant_portion, vertical_grid_count, col_dev)]
    convert_element_type x1 -> x0, local copies, waits for them, and re-layouts: 9.14 us -> none  [on_device(): return (modal_amplitude - mean_coef).astype(jnp.bfloat16)]
    select_n x3 -> x0, other arithmetic: 7.7 us -> none  [the longest x1 7.69 us: on_device(): jnp.take(grouped, station_permutation_map, axis=2)]
  transfers between devices with their start and end apart: 1 -> 0, of which waited for: 1 -> 0; matrix products, arithmetic and copies ran while one was open for 4% -> 0% of each run, Pallas kernels for 0% -> 0%
where the time goes in v1:
time: 185 us; the launch traced here: 182 us
  Pallas kernels  176 us (95%)
  local copies, waits for them, and re-layouts  5.14 us (3%)
    pallas_call x1, Pallas kernels, on_device(): pl.pallas_call(exchange_kernel, out_shape=(jax.ShapeDtypeStruct((mode_cou...  151 us
    pallas_call x1, Pallas kernels, on_device(): pl.pallas_call(regroup_kernel, grid=(devices // step,), out_shape=(jax.Sh...  15.6 us
    pallas_call x1, Pallas kernels, on_device(): pl.pallas_call(centre_kernel, grid=(mode_count // rows,), out_shape=jax.S...  10 us
    unnamed x7, local copies, waits for them, and re-layouts  5.14 us

profile of v1, /device:TPU:1, one launch (start us, length us, event | category | flops | bytes accessed | tf_op | source)
XLA Modules:
  0.0 181.7 jit_solution(13461121478843721738)
XLA Ops:
  0.0 1.1 copy.5.basis
  1.1 15.6 %regroup.1 = (bf16[256,96,128]{2,1,0:T(8,128)(2,1)}, s32[1,128]{1,0:T(1,128)}) custom-call(s32[1024]{0:T(1024)} %perm.1, s32[1]{0:T(128)} %bitcast.mine, s32[256,128]{1,0:T(8,128)} %bitcast.4, bf16[90,32768]{1,0:T(8,128)(2,1)} %bitcast.3), custom_call_target="tpu_custom_call" | custom-call | tf_op jit(solution)/shard_map/regroup/pallas_call | solution.py:154
  16.6 0.0 copy-start
  16.6 2.8 %copy-done = bf16[256,96,128]{2,1,0:T(8,128)(2,1)S(1)} copy-done((bf16[256,96,128]{2,1,0:T(8,128)(2,1)S(1)}, bf16[256,96,128]{2,1,0:T(8,128)(2,1)}, u32[]{:S(2)}) %copy-start) | copy-done | bytes 6291480
  19.4 0.0 copy-start.2
  19.4 0.7 copy-done.2
  20.1 150.9 %exchange.1 = (f32[90,264,128]{2,1,0:T(8,128)}, f32[90,128]{1,0:T(8,128)S(1)}) custom-call(s32[1,128]{1,0:T(1,128)S(1)} %copy-done.2, bf16[16,90,90]{2,1,0:T(8,128)(2,1)S(1)} %copy.5.basis, bf16[256,96,128]{2,1,0:T(8,128)(2,1)S(1)} %copy-done), custom_call_target="tpu_custom_call" | custom-call | tf_op jit(solution)/shard_map/exchange/pallas_call | solution.py:170
  171.0 0.0 copy-start.1
  171.1 0.6 copy-done.1
  171.7 10.0 %centre.1 = bf16[90,256,128]{2,1,0:T(8,128)(2,1)} custom-call(f32[90,264,128]{2,1,0:T(8,128)} %get-tuple-element.11.coef, f32[90,128]{1,0:T(8,128)} %copy-done.1), custom_call_target="tpu_custom_call" | custom-call | tf_op jit(solution)/shard_map/centre/pallas_call | solution.py:192
Async XLA Ops:
  16.6 2.8 %copy-start = (bf16[256,96,128]{2,1,0:T(8,128)(2,1)S(1)}, bf16[256,96,128]{2,1,0:T(8,128)(2,1)}, u32[]{:S(2)}) copy-start(bf16[256,96,128]{2,1,0:T(8,128)(2,1)} %get-tuple-element.10.outbox) | copy-start | bytes 18874372
  19.4 0.7 copy-start.2
  171.0 0.6 copy-start.1

commit v2 on v1

v2 whole, which is shorter than its diff:
```python
import jax
import jax.numpy as jnp
from jax import lax
from jax.experimental import pallas as pl
from jax.experimental.pallas import tpu as pltpu
from jax.sharding import PartitionSpec as P

TILE = 32
LANES = 128
MESH = pl.DeviceIdType.MESH


def place():
    ta, tb = lax.axis_index("ta"), lax.axis_index("tb")
    return ta // 2, ta % 2, tb % 4, tb // 4


def peer(step, sign):
    x, core, y, z = place()
    turn, row = step % 8, step // 8
    dz = jnp.where(turn % 2 == 1, 8 - (turn + 1) // 2, turn // 2 + 1)
    dz = jnp.where(turn == 7, 0, dz)
    near = row < 4
    which = jnp.where(near, 0, (row + 3) % 7 + 1)
    dy = (jnp.where(near, row, (row - 4) // 7) + turn) % 4
    ta = ((x + sign * (which // 2) + 4) % 4) * 2 + (core + which) % 2
    tb = ((z + sign * dz + 8) % 8) * 4 + (y + sign * dy + 4) % 4
    return ta, tb


SELF = 15


def exchange_kernel(
    perm, group, basis, theta, coef, total, field, outbox, inbox, modes, load_sem, send_sem, recv_sem, stage_sem
):
    levels, columns = theta.shape
    classes = basis.shape[0]
    devices = columns // LANES
    ta, tb = lax.axis_index("ta"), lax.axis_index("tb")
    me = ta * 32 + tb

    barrier = pltpu.get_barrier_semaphore()

    def greet(d, carry):
        pl.semaphore_signal(barrier, inc=1, device_id=(ta, (tb + d) % 32), device_id_type=MESH)
        return carry

    lax.fori_loop(1, 32, greet, 0)
    for d in range(1, 8):
        pl.semaphore_signal(barrier, inc=1, device_id=((ta + d) % 8, tb), device_id_type=MESH)

    def load(i, carry):
        tile = theta.at[:, pl.ds(pl.multiple_of(i * LANES, LANES), LANES)]
        pltpu.make_async_copy(tile, field.at[i], load_sem).start()
        return carry

    lax.fori_loop(0, devices, load, 0, unroll=8)

    def gathered(t, rows, dtype, read):
        quarter = lax.broadcasted_iota(jnp.int32, (rows, LANES), 1) // TILE
        zero = jnp.zeros((rows, LANES), dtype)
        groups = [perm[4 * t + k] for k in range(4)]
        parts = [read(lax.shift_right_logical(g, 2)) for g in groups]
        block = zero
        for j in range(4):
            moved = zero
            for h in range(4):
                k = (h + j) % 4
                wanted = 4 * (groups[k] & 3) - 3 * h
                moved = jnp.where(quarter == wanted, parts[k], moved)
            block = block + (pltpu.roll(moved, j * TILE, 1) if j else moved)
        return block

    def regroup(t):
        return gathered(t, levels, jnp.bfloat16, lambda tile: field[tile])

    pltpu.make_async_copy(field, field, load_sem).wait()
    inbox[me, pl.ds(0, levels), :] = regroup(me)

    def fill(step, carry):
        a, b = peer(step, 1)
        t = a * 32 + b

        @pl.when(step != SELF)
        def _():
            outbox[t, pl.ds(0, levels), :] = regroup(t)

        return carry

    def send(step):
        a, b = peer(step, 1)
        t = a * 32 + b

        @pl.when(step != SELF)
        def _():
            pltpu.make_async_remote_copy(
                src_ref=outbox.at[t, pl.ds(0, levels)],
                dst_ref=inbox.at[me, pl.ds(0, levels)],
                send_sem=send_sem,
                recv_sem=recv_sem.at[me],
                device_id=(a, b),
                device_id_type=MESH,
            ).start()

    ahead = 4

    def fill_and_send(step, carry):
        send(step)
        fill(step + ahead, carry)
        return carry

    def send_rest(step, carry):
        send(step)
        return carry

    lax.fori_loop(0, ahead, fill, 0)
    pl.semaphore_wait(barrier, 38)
    for d in range(1, 8):
        pl.semaphore_signal(stage_sem, inc=1, device_id=((ta + d) % 8, tb), device_id_type=MESH)
    lax.fori_loop(0, 32, fill_and_send, 0)
    pl.semaphore_wait(stage_sem, 7)
    lax.fori_loop(32, devices - ahead, fill_and_send, 0)
    lax.fori_loop(devices - ahead, devices, send_rest, 0)

    kind = gathered(me, 1, jnp.int32, lambda tile: group[pl.ds(tile, 1), :])
    for c in range(classes):
        modes[c] = basis[c].astype(jnp.float32).T.astype(jnp.bfloat16)
    total[...] = jnp.zeros_like(total)

    def project(s):
        found = inbox[s, pl.ds(0, levels), :]
        out = jnp.zeros((levels, LANES), jnp.float32)
        for c in range(classes):
            part = jnp.dot(modes[c], found, preferred_element_type=jnp.float32)
            out = jnp.where(kind == c, part, out)
        coef[:, s, :] = out
        total[...] += out

    project(me)

    def receive(step, carry):
        a, b = peer(step, -1)
        s = a * 32 + b

        @pl.when(step != SELF)
        def _():
            here = inbox.at[s, pl.ds(0, levels)]
            pltpu.make_async_copy(here, here, recv_sem.at[s]).wait()
            project(s)

        return carry

    lax.fori_loop(0, devices, receive, 0)
    sent = outbox.at[pl.ds(0, devices - 1), pl.ds(0, levels)]
    pltpu.make_async_copy(sent, sent, send_sem).wait()


def centre_kernel(coef, total, out):
    rows, snaps, _ = out.shape
    first = pl.program_id(0) * rows
    for m in range(rows):
        mean = total[pl.ds(first + m, 1), :] * (1.0 / snaps)
        out[m] = (coef[first + m, pl.ds(0, snaps), :] - mean).astype(out.dtype)


def on_device(theta_cube, station_permutation_map, station_bathymetry_group, baroclinic_basis):
    _, levels, columns = theta_cube.shape
    classes, _, mode_count = baroclinic_basis.shape
    devices = columns // LANES
    snaps = devices
    vmem = pl.BlockSpec(memory_space=pltpu.VMEM)
    coef, total = pl.pallas_call(
        exchange_kernel,
        out_shape=(
            pltpu.VMEM((mode_count, snaps + 8, LANES), jnp.float32),
            pltpu.VMEM((mode_count, LANES), jnp.float32),
        ),
        in_specs=[pl.BlockSpec(memory_space=pltpu.SMEM), vmem, vmem, pl.BlockSpec(memory_space=pl.ANY)],
        out_specs=(vmem, vmem),
        scratch_shapes=[
            pltpu.VMEM((devices, levels, LANES), jnp.bfloat16),
            pltpu.VMEM((devices, 96, LANES), jnp.bfloat16),
            pltpu.VMEM((devices, 96, LANES), jnp.bfloat16),
            pltpu.VMEM((classes, mode_count, levels), jnp.bfloat16),
            pltpu.SemaphoreType.DMA,
            pltpu.SemaphoreType.DMA,
            pltpu.SemaphoreType.DMA((devices,)),
            pltpu.SemaphoreType.REGULAR,
        ],
        compiler_params=pltpu.CompilerParams(
            collective_id=0, has_side_effects=True, vmem_limit_bytes=36 * 2**20
        ),
        name="exchange",
    )(
        station_permutation_map,
        station_bathymetry_group.reshape(columns // LANES, LANES),
        baroclinic_basis,
        theta_cube.reshape(levels, columns),
    )
    rows = 9
    return pl.pallas_call(
        centre_kernel,
        grid=(mode_count // rows,),
        out_shape=jax.ShapeDtypeStruct((mode_count, snaps, LANES), jnp.bfloat16),
        in_specs=[vmem, vmem],
        out_specs=pl.BlockSpec((rows, snaps, LANES), lambda i: (i, 0, 0)),
        compiler_params=pltpu.CompilerParams(vmem_limit_bytes=8 * 2**20),
        name="centre",
    )(pltpu.with_memory_space_constraint(coef, pltpu.VMEM), pltpu.with_memory_space_constraint(total, pltpu.VMEM))


def solution(mesh):
    return jax.shard_map(
        on_device,
        mesh=mesh,
        in_specs=(P(("ta", "tb"), None, None), P(), P(), P()),
        out_specs=P(None, None, ("ta", "tb")),
        check_vma=False,
    )
```

time: 185 us -> 157 us (0.85); the launches traced: 182 us -> 157 us
  Pallas kernels: 176 us -> 155 us
  local copies, waits for them, and re-layouts: 5.14 us -> 2.67 us
    pallas_call x2 -> x1, Pallas kernels: 166 us -> 150 us  [on_device(): pl.pallas_call(exchange_kernel, out_shape=(pltpu.VMEM((mode_count, snaps...]
    pallas_call x1, Pallas kernels: 10 us -> 4.62 us  [on_device(): pl.pallas_call(centre_kernel, grid=(mode_count // rows,), out_shape=jax.S...]
    unnamed x7 -> x5, local copies, waits for them, and re-layouts: 5.14 us -> 2.67 us
where the time goes in v2:
time: 157 us
  Pallas kernels  155 us (99%)
  local copies, waits for them, and re-layouts  2.67 us (2%)
    pallas_call x1, Pallas kernels, on_device(): pl.pallas_call(exchange_kernel, out_shape=(pltpu.VMEM((mode_count, snaps...  150 us
    pallas_call x1, Pallas kernels, on_device(): pl.pallas_call(centre_kernel, grid=(mode_count // rows,), out_shape=jax.S...  4.62 us

profile of v2, /device:TPU:1, one launch (start us, length us, event | category | flops | bytes accessed | tf_op | source)
XLA Modules:
  0.0 157.2 jit_solution(16209662706809361709)
XLA Ops:
  0.0 1.1 copy.5.basis
  1.1 0.0 copy-start
  1.1 0.9 copy-done
  2.0 0.0 copy-start.1
  2.0 0.7 copy-done.1
  2.7 149.9 %exchange.1 = (f32[90,264,128]{2,1,0:T(8,128)S(1)}, f32[90,128]{1,0:T(8,128)S(1)}) custom-call(s32[1024]{0:T(1024)S(1)} %copy-done.1, s32[256,128]{1,0:T(8,128)S(1)} %bitcast.2, bf16[16,90,90]{2,1,0:T(8,128)(2,1)S(1)} %copy.5.basis, bf16[90,32768]{1,0:T(8,128)(2,1)} %bitcast.3), custom_call_target="tpu_custom_call" | custom-call | tf_op jit(solution)/shard_map/exchange/pallas_call | solution.py:173
  152.6 4.6 %centre.1 = bf16[90,256,128]{2,1,0:T(8,128)(2,1)} custom-call(f32[90,264,128]{2,1,0:T(8,128)S(1)} %get-tuple-element.7.coef, f32[90,128]{1,0:T(8,128)S(1)} %get-tuple-element.8.total), custom_call_target="tpu_custom_call" | custom-call | tf_op jit(solution)/shard_map/centre/pallas_call | solution.py:202
Async XLA Ops:
  1.1 0.9 copy-start
  2.0 0.7 copy-start.1

commit v3 on v2

v3 whole, which is shorter than its diff:
```python
import jax
import jax.numpy as jnp
from jax import lax
from jax.experimental import pallas as pl
from jax.experimental.pallas import tpu as pltpu
from jax.sharding import PartitionSpec as P

TILE = 32
LANES = 128
MESH = pl.DeviceIdType.MESH
NEAR = 31


def at(x, core, y, z):
    return ((x + 4) % 4) * 2 + (core + 2) % 2, ((z + 8) % 8) * 4 + (y + 4) % 4


def place():
    ta, tb = lax.axis_index("ta"), lax.axis_index("tb")
    return ta // 2, ta % 2, tb % 4, tb // 4


def peer(step, sign):
    x, core, y, z = place()
    near = step < NEAR
    i = jnp.where(step >= 28, step - 27, step)
    turn, row = i % 8, i // 8
    reach = jnp.where(turn % 2 == 0, row + 1, -row - 1)
    near_z = jnp.where(step >= 28, 0, jnp.where(step >= 24, 4, reach))
    near_y = jnp.where(step >= 24, i % 4, turn // 2)
    far = step - NEAR
    turn, row = far % 8, far // 8
    far_z = jnp.where(turn % 2 == 1, -(turn + 1) // 2, turn // 2 + 1)
    far_z = jnp.where(turn == 7, 0, far_z)
    which = jnp.where(near, 0, row % 7 + 1)
    dz = jnp.where(near, near_z, far_z)
    dy = jnp.where(near, near_y, (row // 7 + turn) % 4)
    ta = ((x + sign * (which // 2) + 4) % 4) * 2 + (core + which) % 2
    tb = ((z + sign * dz + 8) % 8) * 4 + (y + sign * dy + 4) % 4
    return ta, tb


def exchange_kernel(
    perm_in, group_in, basis_in, theta, coef, total,
    perm, group, basis, field, outbox, inbox, modes,
    small_sem, load_sem, send_sem, recv_sem, stage_sem,
):
    levels, columns = theta.shape
    classes = basis_in.shape[1]
    devices = columns // LANES
    ta, tb = lax.axis_index("ta"), lax.axis_index("tb")
    me = ta * 32 + tb
    x, core, y, z = place()
    barrier = pltpu.get_barrier_semaphore()

    def tell(sem, device):
        pl.semaphore_signal(sem, inc=1, device_id=device, device_id_type=MESH)

    fetch_perm = pltpu.make_async_copy(perm_in, perm, small_sem.at[0])
    fetch_perm.start()
    for d in range(4):
        for dz in (1, -1):
            tell(barrier, at(x, core, y + d, z + dz))
    for d in range(1, 8):
        tell(barrier, ((ta + d) % 8, tb))

    def load(i, carry):
        tile = theta.at[:, pl.ds(pl.multiple_of(i * LANES, LANES), LANES)]
        pltpu.make_async_copy(tile, field.at[i], load_sem).start()
        return carry

    lax.fori_loop(0, devices, load, 0, unroll=8)
    fetch_group = pltpu.make_async_copy(group_in, group, small_sem.at[1])
    fetch_basis = pltpu.make_async_copy(basis_in, basis, small_sem.at[2])
    fetch_group.start()
    fetch_basis.start()

    def gathered(t, rows, dtype, read):
        quarter = lax.broadcasted_iota(jnp.int32, (rows, LANES), 1) // TILE
        zero = jnp.zeros((rows, LANES), dtype)
        groups = [perm[4 * t + k] for k in range(4)]
        parts = [read(lax.shift_right_logical(g, 2)) for g in groups]
        block = None
        for j in range(4):
            moved = zero
            for h in range(4):
                k = (h + j) % 4
                wanted = 4 * (groups[k] & 3) - 3 * h
                moved = jnp.where(quarter == wanted, parts[k], moved)
            moved = pltpu.roll(moved, j * TILE, 1) if j else moved
            block = moved if block is None else block + moved
        return block

    def regroup(t):
        return gathered(t, levels, jnp.bfloat16, lambda tile: field[tile])

    def fill(step, carry):
        a, b = peer(step, 1)
        t = a * 32 + b
        outbox[t, pl.ds(0, levels), :] = regroup(t)
        return carry

    def send(step, carry):
        a, b = peer(step, 1)
        t = a * 32 + b
        pltpu.make_async_remote_copy(
            src_ref=outbox.at[t, pl.ds(0, levels)],
            dst_ref=inbox.at[me, pl.ds(0, levels)],
            send_sem=send_sem,
            recv_sem=recv_sem.at[me],
            device_id=(a, b),
            device_id_type=MESH,
        ).start()
        return carry

    ahead = 4

    def send_and_fill(step, carry):
        send(step, carry)
        fill(step + ahead, carry)
        return carry

    fetch_perm.wait()
    pltpu.make_async_copy(field, field, load_sem).wait()
    lax.fori_loop(0, ahead, fill, 0)
    pl.semaphore_wait(barrier, 15)
    for dz in (1, -1):
        tell(stage_sem.at[0], at(x, core, y, z + dz))
    lax.fori_loop(0, 8, send_and_fill, 0)
    pl.semaphore_wait(stage_sem.at[0], 2)
    for dz in (2, -2):
        tell(stage_sem.at[1], at(x, core, y, z + dz))
    lax.fori_loop(8, 16, send_and_fill, 0)
    pl.semaphore_wait(stage_sem.at[1], 2)
    for d in range(1, 8):
        tell(stage_sem.at[2], ((ta + d) % 8, tb))
    lax.fori_loop(16, NEAR, send_and_fill, 0)
    pl.semaphore_wait(stage_sem.at[2], 7)
    lax.fori_loop(NEAR, devices - 1 - ahead, send_and_fill, 0)
    lax.fori_loop(devices - 1 - ahead, devices - 1, send, 0)

    inbox[me, pl.ds(0, levels), :] = regroup(me)
    fetch_group.wait()
    kind = gathered(me, 1, jnp.int32, lambda tile: group[pl.ds(tile, 1), :])
    kind = jnp.concatenate([kind, kind], axis=1)
    fetch_basis.wait()
    for c in range(classes):
        modes[c] = basis[:, c, :].astype(jnp.float32).T.astype(jnp.bfloat16)
    total[...] = jnp.zeros_like(total)

    def project(first, second):
        found = jnp.concatenate([inbox[first, pl.ds(0, levels), :], inbox[second, pl.ds(0, levels), :]], axis=1)
        out = jnp.zeros((total.shape[0], 2 * LANES), jnp.float32)
        for c in range(classes):
            part = jnp.dot(modes[c], found, preferred_element_type=jnp.float32)
            out = jnp.where(kind == c, part, out)
        coef[:, first, :] = out[:, :LANES]
        coef[:, second, :] = out[:, LANES:]
        total[...] += out[:, :LANES] + out[:, LANES:]

    def arrived(step):
        a, b = peer(step, -1)
        s = a * 32 + b
        here = inbox.at[s, pl.ds(0, levels)]
        pltpu.make_async_copy(here, here, recv_sem.at[s]).wait()
        return s

    project(me, arrived(0))

    def receive(i, carry):
        first = arrived(2 * i + 1)
        project(first, arrived(2 * i + 2))
        return carry

    lax.fori_loop(0, (devices - 2) // 2, receive, 0)
    sent = outbox.at[pl.ds(0, devices - 1), pl.ds(0, levels)]
    pltpu.make_async_copy(sent, sent, send_sem).wait()


def centre_kernel(coef, total, out):
    rows, snaps, _ = out.shape
    first = pl.program_id(0) * rows
    for m in range(rows):
        mean = total[pl.ds(first + m, 1), :] * (1.0 / snaps)
        out[m] = (coef[first + m, pl.ds(0, snaps), :] - mean).astype(out.dtype)


def on_device(theta_cube, station_permutation_map, station_bathymetry_group, baroclinic_basis):
    _, levels, columns = theta_cube.shape
    classes, _, mode_count = baroclinic_basis.shape
    devices = columns // LANES
    snaps = devices
    vmem = pl.BlockSpec(memory_space=pltpu.VMEM)
    hbm = pl.BlockSpec(memory_space=pl.ANY)
    coef, total = pl.pallas_call(
        exchange_kernel,
        out_shape=(
            pltpu.VMEM((mode_count, snaps + 8, LANES), jnp.float32),
            pltpu.VMEM((mode_count, LANES), jnp.float32),
        ),
        in_specs=[hbm] * 4,
        out_specs=(vmem, vmem),
        scratch_shapes=[
            pltpu.SMEM((columns // TILE,), jnp.int32),
            pltpu.VMEM((devices, LANES), jnp.int32),
            pltpu.VMEM((levels, classes, mode_count), jnp.bfloat16),
            pltpu.VMEM((devices, levels, LANES), jnp.bfloat16),
            pltpu.VMEM((devices, 96, LANES), jnp.bfloat16),
            pltpu.VMEM((devices, 96, LANES), jnp.bfloat16),
            pltpu.VMEM((classes, mode_count, levels), jnp.bfloat16),
            pltpu.SemaphoreType.DMA((3,)),
            pltpu.SemaphoreType.DMA,
            pltpu.SemaphoreType.DMA,
            pltpu.SemaphoreType.DMA((devices,)),
            pltpu.SemaphoreType.REGULAR((3,)),
        ],
        compiler_params=pltpu.CompilerParams(
            collective_id=0, has_side_effects=True, vmem_limit_bytes=36 * 2**20
        ),
        name="exchange",
    )(*(pltpu.with_memory_space_constraint(a, pltpu.HBM) for a in (
        station_permutation_map,
        station_bathymetry_group.reshape(columns // LANES, LANES),
        baroclinic_basis.transpose(1, 0, 2),
        theta_cube.reshape(levels, columns),
    )))
    rows = 9
    return pl.pallas_call(
        centre_kernel,
        grid=(mode_count // rows,),
        out_shape=jax.ShapeDtypeStruct((mode_count, snaps, LANES), jnp.bfloat16),
        in_specs=[vmem, vmem],
        out_specs=pl.BlockSpec((rows, snaps, LANES), lambda i: (i, 0, 0)),
        compiler_params=pltpu.CompilerParams(vmem_limit_bytes=8 * 2**20),
        name="centre",
    )(pltpu.with_memory_space_constraint(coef, pltpu.VMEM), pltpu.with_memory_space_constraint(total, pltpu.VMEM))


def solution(mesh):
    return jax.shard_map(
        on_device,
        mesh=mesh,
        in_specs=(P(("ta", "tb"), None, None), P(), P(), P()),
        out_specs=P(None, None, ("ta", "tb")),
        check_vma=False,
    )
```

time: 157 us -> 150 us (0.955)
  Pallas kernels: 155 us -> 150 us
  local copies, waits for them, and re-layouts: 2.67 us -> 0 us
    pallas_call x1, Pallas kernels: 150 us -> 145 us  [on_device(): pl.pallas_call(exchange_kernel, out_shape=(pltpu.VMEM((mode_count, snaps...]
    unnamed x5 -> x0, local copies, waits for them, and re-layouts: 2.67 us -> none
where the time goes in v3:
time: 150 us
  Pallas kernels  150 us (100%)
    pallas_call x1, Pallas kernels, on_device(): pl.pallas_call(exchange_kernel, out_shape=(pltpu.VMEM((mode_count, snaps...  145 us
    pallas_call x1, Pallas kernels, on_device(): pl.pallas_call(centre_kernel, grid=(mode_count // rows,), out_shape=jax.S...  4.62 us

profile of v3, /device:TPU:1, one launch (start us, length us, event | category | flops | bytes accessed | tf_op | source)
XLA Modules:
  0.0 150.1 jit_solution(1715285368506249542)
XLA Ops:
  0.0 145.5 %exchange.1 = (f32[90,264,128]{2,1,0:T(8,128)S(1)}, f32[90,128]{1,0:T(8,128)S(1)}) custom-call(s32[1024]{0:T(1024)} %perm_in.1, s32[256,128]{1,0:T(8,128)} %bitcast.5, bf16[90,16,90]{2,1,0:T(8,128)(2,1)} %bitcast.4, bf16[90,32768]{1,0:T(8,128)(2,1)} %bitcast.3), custom_call_target="tpu_custom_call" | custom-call | tf_op jit(solution)/shard_map/exchange/pallas_call | solution.py:195
  145.5 4.6 %centre.1 = bf16[90,256,128]{2,1,0:T(8,128)(2,1)} custom-call(f32[90,264,128]{2,1,0:T(8,128)S(1)} %get-tuple-element.7.coef, f32[90,128]{1,0:T(8,128)S(1)} %get-tuple-element.8.total), custom_call_target="tpu_custom_call" | custom-call | tf_op jit(solution)/shard_map/centre/pallas_call | solution.py:228

commit v4 on v3

--- a/solution.py
+++ b/solution.py
@@ -57,19 +57,15 @@
         pl.semaphore_signal(sem, inc=1, device_id=device, device_id_type=MESH)
 
     fetch_perm = pltpu.make_async_copy(perm_in, perm, small_sem.at[0])
+    load = pltpu.make_async_copy(theta, field, load_sem)
     fetch_perm.start()
+    load.start()
     for d in range(4):
         for dz in (1, -1):
             tell(barrier, at(x, core, y + d, z + dz))
     for d in range(1, 8):
         tell(barrier, ((ta + d) % 8, tb))
 
-    def load(i, carry):
-        tile = theta.at[:, pl.ds(pl.multiple_of(i * LANES, LANES), LANES)]
-        pltpu.make_async_copy(tile, field.at[i], load_sem).start()
-        return carry
-
-    lax.fori_loop(0, devices, load, 0, unroll=8)
     fetch_group = pltpu.make_async_copy(group_in, group, small_sem.at[1])
     fetch_basis = pltpu.make_async_copy(basis_in, basis, small_sem.at[2])
     fetch_group.start()
@@ -92,7 +88,7 @@
         return block
 
     def regroup(t):
-        return gathered(t, levels, jnp.bfloat16, lambda tile: field[tile])
+        return gathered(t, levels, jnp.bfloat16, lambda tile: field[:, pl.ds(tile * LANES, LANES)])
 
     def fill(step, carry):
         a, b = peer(step, 1)
@@ -113,7 +109,7 @@
         ).start()
         return carry
 
-    ahead = 4
+    ahead = 2
 
     def send_and_fill(step, carry):
         send(step, carry)
@@ -121,7 +117,7 @@
         return carry
 
     fetch_perm.wait()
-    pltpu.make_async_copy(field, field, load_sem).wait()
+    load.wait()
     lax.fori_loop(0, ahead, fill, 0)
     pl.semaphore_wait(barrier, 15)
     for dz in (1, -1):
@@ -177,12 +173,20 @@
     pltpu.make_async_copy(sent, sent, send_sem).wait()
 
 
-def centre_kernel(coef, total, out):
-    rows, snaps, _ = out.shape
-    first = pl.program_id(0) * rows
-    for m in range(rows):
-        mean = total[pl.ds(first + m, 1), :] * (1.0 / snaps)
-        out[m] = (coef[first + m, pl.ds(0, snaps), :] - mean).astype(out.dtype)
+def centre_kernel(coef, total, out, rounded, sem):
+    modes, snaps, _ = out.shape
+    rows = 2
+
+    def part(i, carry):
+        for m in range(rows):
+            mean = total[pl.ds(i * rows + m, 1), :] * (1.0 / snaps)
+            rounded[i * rows + m] = (coef[i * rows + m, pl.ds(0, snaps), :] - mean).astype(out.dtype)
+        here = pl.ds(i * rows, rows)
+        pltpu.make_async_copy(rounded.at[here], out.at[here], sem).start()
+        return carry
+
+    lax.fori_loop(0, modes // rows, part, 0)
+    pltpu.make_async_copy(rounded, out, sem).wait()
 
 
 def on_device(theta_cube, station_permutation_map, station_bathymetry_group, baroclinic_basis):
@@ -204,7 +208,7 @@
             pltpu.SMEM((columns // TILE,), jnp.int32),
             pltpu.VMEM((devices, LANES), jnp.int32),
             pltpu.VMEM((levels, classes, mode_count), jnp.bfloat16),
-            pltpu.VMEM((devices, levels, LANES), jnp.bfloat16),
+            pltpu.VMEM((levels, columns), jnp.bfloat16),
             pltpu.VMEM((devices, 96, LANES), jnp.bfloat16),
             pltpu.VMEM((devices, 96, LANES), jnp.bfloat16),
             pltpu.VMEM((classes, mode_count, levels), jnp.bfloat16),
@@ -224,14 +228,13 @@
         baroclinic_basis.transpose(1, 0, 2),
         theta_cube.reshape(levels, columns),
     )))
-    rows = 9
     return pl.pallas_call(
         centre_kernel,
-        grid=(mode_count // rows,),
         out_shape=jax.ShapeDtypeStruct((mode_count, snaps, LANES), jnp.bfloat16),
         in_specs=[vmem, vmem],
-        out_specs=pl.BlockSpec((rows, snaps, LANES), lambda i: (i, 0, 0)),
-        compiler_params=pltpu.CompilerParams(vmem_limit_bytes=8 * 2**20),
+        out_specs=hbm,
+        scratch_shapes=[pltpu.VMEM((mode_count, snaps, LANES), jnp.bfloat16), pltpu.SemaphoreType.DMA],
+        compiler_params=pltpu.CompilerParams(vmem_limit_bytes=12 * 2**20),
         name="centre",
     )(pltpu.with_memory_space_constraint(coef, pltpu.VMEM), pltpu.with_memory_space_constraint(total, pltpu.VMEM))
 

time: 150 us -> 147 us (0.980)
  Pallas kernels: 150 us -> 147 us
    pallas_call x1, Pallas kernels: 4.62 us -> 2.51 us  [on_device(): pl.pallas_call(centre_kernel, out_shape=jax.ShapeDtypeStruct((mode_count,...]
where the time goes in v4:
time: 147 us
  Pallas kernels  147 us (100%)
    pallas_call x1, Pallas kernels, on_device(): pl.pallas_call(exchange_kernel, out_shape=(pltpu.VMEM((mode_count, snaps...  145 us

profile of v4, /device:TPU:1, one launch (start us, length us, event | category | flops | bytes accessed | tf_op | source)
XLA Modules:
  0.0 147.3 jit_solution(7548378355568513407)
XLA Ops:
  0.0 144.8 %exchange.1 = (f32[90,264,128]{2,1,0:T(8,128)S(1)}, f32[90,128]{1,0:T(8,128)S(1)}) custom-call(s32[1024]{0:T(1024)} %perm_in.1, s32[256,128]{1,0:T(8,128)} %bitcast.5, bf16[90,16,90]{2,1,0:T(8,128)(2,1)} %bitcast.4, bf16[90,32768]{1,0:T(8,128)(2,1)} %bitcast.3), custom_call_target="tpu_custom_call" | custom-call | tf_op jit(solution)/shard_map/exchange/pallas_call | solution.py:199
  144.8 2.5 %centre.1 = bf16[90,256,128]{2,1,0:T(8,128)(2,1)} custom-call(f32[90,264,128]{2,1,0:T(8,128)S(1)} %get-tuple-element.7.coef, f32[90,128]{1,0:T(8,128)S(1)} %get-tuple-element.8.total), custom_call_target="tpu_custom_call" | custom-call | tf_op jit(solution)/shard_map/centre/pallas_call | solution.py:231

commit v5 on v4

--- a/solution.py
+++ b/solution.py
@@ -29,12 +29,17 @@
     near_z = jnp.where(step >= 28, 0, jnp.where(step >= 24, 4, reach))
     near_y = jnp.where(step >= 24, i % 4, turn // 2)
     far = step - NEAR
-    turn, row = far % 8, far // 8
-    far_z = jnp.where(turn % 2 == 1, -(turn + 1) // 2, turn // 2 + 1)
+    late, k, m = far >= 184, far - 184, far % 46
+    full = m < 16
+    pick = jnp.where(late, (k % 10 // 2 + 1) % 5, (m - 16) // 6)
+    pick = pick + jnp.where(pick >= 3, 3, 1)
+    which = jnp.where(near, 0, jnp.where(late, pick, jnp.where(full, 4 + m // 8, pick)))
+    turn = jnp.where(late, k % 2, jnp.where(full, m % 8, 2 + (m - 16) % 6))
+    far_z = jnp.where(turn % 2 == 1, -((turn + 1) // 2), turn // 2 + 1)
     far_z = jnp.where(turn == 7, 0, far_z)
-    which = jnp.where(near, 0, row % 7 + 1)
+    late_y = jnp.where(k // 10 == 3, 0, jnp.where(k // 10 == 2, 3, 2 - k // 10))
     dz = jnp.where(near, near_z, far_z)
-    dy = jnp.where(near, near_y, (row // 7 + turn) % 4)
+    dy = jnp.where(near, near_y, jnp.where(late, late_y, (far // 46 + turn) % 4))
     ta = ((x + sign * (which // 2) + 4) % 4) * 2 + (core + which) % 2
     tb = ((z + sign * dz + 8) % 8) * 4 + (y + sign * dy + 4) % 4
     return ta, tb

time: 147 us -> 164 us (1.12)
  Pallas kernels: 147 us -> 163 us
    pallas_call x1, Pallas kernels: 145 us -> 161 us  [on_device(): pl.pallas_call(exchange_kernel, out_shape=(pltpu.VMEM((mode_count, snaps...]
where the time goes in v5:
time: 164 us; the launch traced here: 163 us
  Pallas kernels  163 us (99%)
    pallas_call x1, Pallas kernels, on_device(): pl.pallas_call(exchange_kernel, out_shape=(pltpu.VMEM((mode_count, snaps...  161 us

profile of v5, /device:TPU:1, one launch (start us, length us, event | category | flops | bytes accessed | tf_op | source)
XLA Modules:
  0.0 163.4 jit_solution(18442942684655806520)
XLA Ops:
  0.0 160.9 %exchange.1 = (f32[90,264,128]{2,1,0:T(8,128)S(1)}, f32[90,128]{1,0:T(8,128)S(1)}) custom-call(s32[1024]{0:T(1024)} %perm_in.1, s32[256,128]{1,0:T(8,128)} %bitcast.5, bf16[90,16,90]{2,1,0:T(8,128)(2,1)} %bitcast.4, bf16[90,32768]{1,0:T(8,128)(2,1)} %bitcast.3), custom_call_target="tpu_custom_call" | custom-call | tf_op jit(solution)/shard_map/exchange/pallas_call | solution.py:204
  160.9 2.5 %centre.1 = bf16[90,256,128]{2,1,0:T(8,128)(2,1)} custom-call(f32[90,264,128]{2,1,0:T(8,128)S(1)} %get-tuple-element.7.coef, f32[90,128]{1,0:T(8,128)S(1)} %get-tuple-element.8.total), custom_call_target="tpu_custom_call" | custom-call | tf_op jit(solution)/shard_map/centre/pallas_call | solution.py:236
